TPU v7x, 32 devices: a whole 2x2x4 slice. The times are simulated.
32 devices in a mesh: section: 4 (over y, core), tensor: 2 (over x), dp: 4 (over z).
Axes of the slice: x: 2, y: 2, z: 4, core: 2. Of those that a mesh axis runs over, the one named last changes fastest.
Arguments:
- acts: bfloat16 [4, 8, 256, 2048], P('section', 'dp', 'tensor'), parts along dimension 1, may hold values from -6 to 6
- fresh: bfloat16 [8, 256, 2048], P('dp', 'tensor'), parts along dimension 0, may hold values from -6 to 6
- order: int32 [4, 2], P('section'), may hold values from 0 to 1
- ln_gain: float32 [4, 2048], P('section'), may hold values from 0.1 to 1.9
- ln_bias: float32 [4, 2048], P('section'), may hold values from -3 to 3
- wqkv: bfloat16 [4, 2048, 6144], P('section', None, 'tensor'), may hold values from -4 to 4
- wo: bfloat16 [4, 2048, 2048], P('section', 'tensor'), may hold values from -0.125 to 0.125
Outputs:
- section_out: bfloat16 [8, 4, 256, 2048], P('dp', 'section', 'tensor'), parts along dimension 0
- held: bfloat16 [4, 8, 256, 2048], P('section', 'dp', 'tensor'), parts along dimension 1
There are 4 independent parts, one for each index of `dp`. A program takes and returns all parts, laid end to end along the dimension named above; an argument that names none is the same for every part. Nothing has to cross between parts.
All inputs are finite; a program needn't handle non-finite values.
Results may differ from a plain program's by a relative error of at most 0.017.
Values may be sent and summed in bfloat16 or wider, within the bound.
A program may use at most 64 MiB of HBM per device.

v0:
```python
import functools
import math

import jax
import jax.numpy as jnp
from jax import lax
from jax.experimental import pallas as pl
from jax.experimental.pallas import tpu as pltpu
from jax.sharding import PartitionSpec as P

HD = 128
EPS = 1e-06
CHUNK = 512
TILE = 1024
NORM_ROWS = 16
PIECE = 32
MESH = pl.DeviceIdType.MESH


def fitting(most, size):
    return math.gcd(most, size)


def relay(
    acts, fresh, order, gain, bias, w_in, w_out, out, held,
    slots, fresh_v, wi, wo, xs, h, hs, acc, qkv, mixed, part, got, arr,
    acts_sem, fresh_sem, wi_sem, wo_sem,
    ag_send, ag_recv, rs_send, rs_recv, hop_send, hop_recv,
):
    ticks, rows, width = fresh.shape
    n_slots = acts.shape[1]
    peers = lax.axis_size("tensor")
    sections = lax.axis_size("section")
    me = lax.axis_index("tensor")
    sec = lax.axis_index("section")
    seq = rows * peers
    heads = wi.shape[1] // (3 * HD)
    chunk = fitting(CHUNK, width)
    n_chunks = width // chunk
    wi_tile = fitting(TILE, wi.shape[1])
    n_tiles = wi.shape[1] // wi_tile
    has_prev = sec > 0
    has_next = sec < sections - 1

    def span(c):
        return pl.ds(c * chunk, chunk)

    def acts_copy(c):
        return pltpu.make_async_copy(acts.at[0, :, :, span(c)], slots.at[:, :, span(c)], acts_sem.at[c])

    for c in range(n_chunks):
        acts_copy(c).start()

    def wi_copy(i):
        cols = pl.ds(i * wi_tile, wi_tile)
        return pltpu.make_async_copy(w_in.at[0, :, cols], wi.at[:, cols], wi_sem.at[i])

    for i in range(n_tiles):
        wi_copy(i).start()
    load_wo = pltpu.make_async_copy(w_out.at[0], wo, wo_sem)
    load_wo.start()
    load_fresh = pltpu.make_async_copy(fresh, fresh_v, fresh_sem)
    load_fresh.start()

    barrier = pltpu.get_barrier_semaphore()
    for d in range(1, peers):
        pl.semaphore_signal(
            barrier, inc=1, device_id={"tensor": lax.rem(me + d, peers)}, device_id_type=MESH
        )

    @pl.when(has_prev)
    def _():
        pl.semaphore_signal(barrier, inc=1, device_id={"section": sec - 1}, device_id_type=MESH)

    @pl.when(has_next)
    def _():
        pl.semaphore_signal(barrier, inc=1, device_id={"section": sec + 1}, device_id_type=MESH)

    def ag_copy(t, d, c):
        src, dst = (xs.at[t, 0], xs.at[t, d]) if t else (hs.at[0], hs.at[d])
        return pltpu.make_async_remote_copy(
            src_ref=src.at[:, span(c)],
            dst_ref=dst.at[:, span(c)],
            send_sem=ag_send.at[t, d - 1, c],
            recv_sem=ag_recv.at[t, d - 1, c],
            device_id={"tensor": lax.rem(me + d, peers)},
            device_id_type=MESH,
        )

    def rs_copy(t, d, c):
        return pltpu.make_async_remote_copy(
            src_ref=part.at[t, d, :, span(c)],
            dst_ref=got.at[t, d - 1, :, span(c)],
            send_sem=rs_send.at[t, d - 1, c],
            recv_sem=rs_recv.at[t, d - 1, c],
            device_id={"tensor": lax.rem(me - d + peers, peers)},
            device_id_type=MESH,
        )

    def hop_copy(t, c):
        return pltpu.make_async_remote_copy(
            src_ref=out.at[t, 0, :, span(c)],
            dst_ref=arr.at[t, :, span(c)],
            send_sem=hop_send.at[t, c],
            recv_sem=hop_recv.at[t, c],
            device_id={"section": lax.rem(sec + 1, sections)},
            device_id_type=MESH,
        )

    def pieces(step):
        for i in range(rows // PIECE):
            step(pl.ds(i * PIECE, PIECE))

    def offer(t, c):
        chosen = order[0, t]

        def step(r):
            x = slots[0, r, span(c)].astype(jnp.float32)
            for k in range(1, n_slots):
                x = jnp.where(chosen == k, slots[k, r, span(c)].astype(jnp.float32), x)
            xs[t, 0, r, span(c)] = x.astype(jnp.bfloat16)

        pieces(step)

    def send_offer(t, c):
        for d in range(1, peers):
            ag_copy(t, d, c).start()

    def norm(t, d):
        into = h if t else hs.at[d]
        g = gain[0:1, :]
        b = bias[0:1, :]

        def one(i, carry):
            r = pl.ds(pl.multiple_of(i * NORM_ROWS, NORM_ROWS), NORM_ROWS)
            values = xs[t, d, r, :].astype(jnp.float32)
            centred = values - jnp.mean(values, axis=-1, keepdims=True)
            spread = jnp.mean(centred * centred, axis=-1, keepdims=True)
            into[r, :] = (centred * lax.rsqrt(spread + EPS) * g + b).astype(jnp.bfloat16)
            return carry

        lax.fori_loop(0, rows // NORM_ROWS, one, 0, unroll=2)

    def project(d, first):
        rows_in = hs.at[0] if first else h
        for i in range(n_tiles):
            if first:
                wi_copy(i).wait()
            cols = pl.ds(i * wi_tile, wi_tile)
            y = jnp.dot(rows_in[...], wi[:, cols], preferred_element_type=jnp.float32)
            qkv[d * rows:(d + 1) * rows, cols] = y.astype(jnp.bfloat16)

    def project_chunk(d, c):
        for i in range(n_tiles):
            cols = pl.ds(i * wi_tile, wi_tile)
            y = jnp.dot(
                hs[d, :, span(c)], wi[span(c), cols], preferred_element_type=jnp.float32
            )
            if c:
                y = acc[:, cols] + y
            if c + 1 < n_chunks:
                acc[:, cols] = y
            else:
                qkv[d * rows:(d + 1) * rows, cols] = y.astype(jnp.bfloat16)

    scale = math.log2(math.e) / math.sqrt(HD)

    def attend(t, d):
        r = slice(d * rows, (d + 1) * rows)
        for n in range(heads):
            base = n * 3 * HD
            q = qkv[r, base:base + HD]
            k = qkv[:, base + HD:base + 2 * HD]
            v = qkv[:, base + 2 * HD:base + 3 * HD]
            s = lax.dot_general(q, k, (((1,), (1,)), ((), ())), preferred_element_type=jnp.float32)
            e = jnp.exp2((s - jnp.max(s, axis=-1, keepdims=True)) * scale)
            total = jnp.sum(e, axis=-1, keepdims=True)
            y = jnp.dot(e.astype(jnp.bfloat16), v, preferred_element_type=jnp.float32)
            mixed[:, n * HD:(n + 1) * HD] = (y / total).astype(jnp.bfloat16)

        for c in range(n_chunks):
            y = jnp.dot(mixed[...], wo[:, span(c)], preferred_element_type=jnp.float32)
            part[t, d, :, span(c)] = y.astype(jnp.bfloat16)
            if d:
                rs_copy(t, d, c).start()

    def finish(t, c):
        for d in range(1, peers):
            rs_copy(t, d, c).wait_recv()

        def step(r):
            total = part[t, 0, r, span(c)].astype(jnp.float32)
            for d in range(1, peers):
                total = total + got[t, d - 1, r, span(c)].astype(jnp.float32)
            x = xs[t, 0, r, span(c)].astype(jnp.float32)
            out[t, 0, r, span(c)] = (x + total).astype(jnp.bfloat16)

        pieces(step)

        @pl.when(has_next)
        def _():
            hop_copy(t, c).start()

    def take(t, c):
        chosen = order[0, t]
        kept = slots if t + 1 < ticks else held.at[0]

        @pl.when(has_prev)
        def _():
            hop_copy(t, c).wait_recv()

        def step(r, source):
            new = source[t, r, span(c)].astype(jnp.float32)
            for k in range(n_slots):
                old = slots[k, r, span(c)].astype(jnp.float32)
                kept[k, r, span(c)] = jnp.where(chosen == k, new, old).astype(jnp.bfloat16)

        @pl.when(has_prev)
        def _():
            pieces(functools.partial(step, source=arr))

        @pl.when(jnp.logical_not(has_prev))
        def _():
            pieces(functools.partial(step, source=fresh_v))

    for c in range(n_chunks):
        acts_copy(c).wait()
        offer(0, c)
    norm(0, 0)
    pl.semaphore_wait(
        barrier, peers - 1 + has_prev.astype(jnp.int32) + has_next.astype(jnp.int32)
    )
    for c in range(n_chunks):
        send_offer(0, c)

    for t in range(ticks):
        if t:
            norm(t, 0)
        project(0, t == 0)
        for d in range(1, peers):
            for c in range(n_chunks):
                ag_copy(t, d, c).wait_recv()
                if t == 0:
                    project_chunk(d, c)
            if t:
                norm(t, d)
                project(d, False)
        if t == 0:
            load_wo.wait()
        for d in [*range(1, peers), 0]:
            attend(t, d)
        if t == 0:
            load_fresh.wait()
        lag = 1
        for step in range(n_chunks + lag):
            if step < n_chunks:
                finish(t, step)
            if step >= lag:
                take(t, step - lag)
                if t + 1 < ticks:
                    offer(t + 1, step - lag)
                    send_offer(t + 1, step - lag)

    for t in range(ticks):
        for c in range(n_chunks):
            for d in range(1, peers):
                ag_copy(t, d, c).wait_send()
                rs_copy(t, d, c).wait_send()

            @pl.when(has_next)
            def _():
                hop_copy(t, c).wait_send()


def pin(*xs):
    return [pltpu.with_memory_space_constraint(x, pltpu.HBM) for x in xs]


def body(acts, fresh, order, ln_gain, ln_bias, wqkv, wo):
    ticks, rows, width = fresh.shape
    n_slots = acts.shape[1]
    peers = lax.axis_size("tensor")
    seq = rows * peers
    n_chunks = width // fitting(CHUNK, width)
    inner = wo.shape[1]
    wide = wqkv.shape[2]
    bf = jnp.bfloat16
    dma = pltpu.SemaphoreType.DMA
    anywhere = pl.BlockSpec(memory_space=pl.ANY)
    vmem = pl.BlockSpec(memory_space=pltpu.VMEM)
    smem = pl.BlockSpec(memory_space=pltpu.SMEM)
    return pl.pallas_call(
        relay,
        out_shape=(
            pltpu.VMEM((ticks, 1, rows, width), bf),
            pltpu.VMEM((1, n_slots, rows, width), bf),
        ),
        in_specs=[anywhere, anywhere, smem, vmem, vmem, anywhere, anywhere],
        out_specs=(vmem, vmem),
        scratch_shapes=[
            pltpu.VMEM((n_slots, rows, width), bf),
            pltpu.VMEM((ticks, rows, width), bf),
            pltpu.VMEM((width, wide), bf),
            pltpu.VMEM((inner, width), bf),
            pltpu.VMEM((ticks, peers, rows, width), bf),
            pltpu.VMEM((rows, width), bf),
            pltpu.VMEM((peers, rows, width), bf),
            pltpu.VMEM((rows, wide), jnp.float32),
            pltpu.VMEM((seq, wide), bf),
            pltpu.VMEM((rows, inner), bf),
            pltpu.VMEM((ticks, peers, rows, width), bf),
            pltpu.VMEM((ticks, peers - 1, rows, width), bf),
            pltpu.VMEM((ticks, rows, width), bf),
            dma((n_chunks,)),
            dma,
            dma((wide // fitting(TILE, wide),)),
            dma,
            dma((ticks, peers - 1, n_chunks)),
            dma((ticks, peers - 1, n_chunks)),
            dma((ticks, peers - 1, n_chunks)),
            dma((ticks, peers - 1, n_chunks)),
            dma((ticks, n_chunks)),
            dma((ticks, n_chunks)),
        ],
        compiler_params=pltpu.CompilerParams(
            collective_id=0, has_side_effects=True, vmem_limit_bytes=52 * 1024 * 1024
        ),
    )(*pin(acts, fresh), order, ln_gain, ln_bias, *pin(wqkv, wo))


def solution(mesh):
    return jax.shard_map(
        body,
        mesh=mesh,
        in_specs=(
            P("section", "dp", "tensor", None),
            P("dp", "tensor", None),
            P("section", None),
            P("section", None),
            P("section", None),
            P("section", None, "tensor"),
            P("section", "tensor", None),
        ),
        out_specs=(P("dp", "section", "tensor", None), P("section", "dp", "tensor", None)),
        check_vma=False,
    )
```

profile of v0, /device:TPU:0, one launch (start us, length us, event | category | flops | bytes accessed | tf_op | source)
XLA Modules:
  0.0 64.6 jit_solution(5940965348323930031)
XLA Ops:
  0.6 62.1 %shard_map.86 = (bf16[2,1,128,2048]{3,2,1,0:T(8,128)(2,1)S(1)}, bf16[1,2,128,2048]{3,2,1,0:T(8,128)(2,1)S(1)}) custom-call(bf16[1,2,128,2048]{3,2,1,0:T(8,128)(2,1)} %acts.1, bf16[2,128,2048]{2,1,0:T(8,128)(2,1)} %fresh.1, s32[1,2]{1,0:T(1,128)} %order.1, f32[1,2048]{1,0:T(1,128)} %gain.1, f32[1,2048]{1,0:T(1,128)} %bias.1, bf16[1,2048,3072]{2,1,0:T(8,128)(2,1)} %w_in.1, ...), custom_call_target="tpu_custom_call" | custom-call | tf_op jit(solution)/shard_map/pallas_call | solution.py:292
  62.7 1.0 %copy.11 = bf16[2,1,128,2048]{3,2,1,0:T(8,128)(2,1)} copy(bf16[2,1,128,2048]{3,2,1,0:T(8,128)(2,1)S(1)} %get-tuple-element.2) | data formatting | bytes 2097152
  63.7 1.0 %copy.12 = bf16[1,2,128,2048]{3,2,1,0:T(8,128)(2,1)} copy(bf16[1,2,128,2048]{3,2,1,0:T(8,128)(2,1)S(1)} %get-tuple-element.3) | data formatting | bytes 2097152
where the time goes:
time: 64.9 us; the launch traced here: 64.6 us
  Pallas kernels  62.1 us (96%)
  local copies, waits for them, and re-layouts  1.94 us (3%)
    pallas_call x1, Pallas kernels, body(): pl.pallas_call(relay, out_shape=(pltpu.VMEM((ticks, 1, rows, width), bf),...  62.1 us
    unnamed x2, local copies, waits for them, and re-layouts  1.94 us

commit v1 on v0

v1 whole, which is shorter than its diff:
```python
import functools
import math

import jax
import jax.numpy as jnp
from jax import lax
from jax.experimental import pallas as pl
from jax.experimental.pallas import tpu as pltpu
from jax.sharding import PartitionSpec as P

HD = 128
EPS = 1e-06
CHUNK = 512
TILE = 1024
NORM_ROWS = 16
PIECE = 32
MESH = pl.DeviceIdType.MESH


def fitting(most, size):
    return math.gcd(most, size)


def rs_spans(width):
    chunk = fitting(CHUNK, width)
    half = fitting(chunk // 2, width)
    sizes = [chunk] * (width // chunk - 1) + [half] * (chunk // half)
    return [(sum(sizes[:i]), size) for i, size in enumerate(sizes)]


def relay(
    acts, fresh, order_h, gain_h, bias_h, w_in, w_out, out, held,
    order, gain, bias, slots, fresh_v, wi, wo, xs, hs, acc, qkv, mixed, part, got, arr,
    small_sem, acts_sem, fresh_sem, wi_sem, wo_sem,
    ag_send, ag_recv, rs_send, rs_recv, hop_send, hop_recv, turn,
):
    ticks, rows, width = fresh.shape
    n_slots = acts.shape[1]
    peers = lax.axis_size("tensor")
    sections = lax.axis_size("section")
    me = lax.axis_index("tensor")
    sec = lax.axis_index("section")
    heads = wi.shape[1] // (3 * HD)
    chunk = fitting(CHUNK, width)
    n_chunks = width // chunk
    wi_tile = fitting(TILE, wi.shape[1])
    n_tiles = wi.shape[1] // wi_tile
    has_prev = sec > 0
    has_next = sec < sections - 1
    late = lax.rem(sec, 2) == 1
    early = jnp.logical_not(late)
    leads = early & has_next
    parts = rs_spans(width)
    n_parts = len(parts)

    def span(c):
        return pl.ds(c * chunk, chunk)

    def part_span(c):
        return pl.ds(*parts[c])

    barrier = pltpu.get_barrier_semaphore()
    for d in range(1, peers):
        pl.semaphore_signal(
            barrier, inc=1, device_id={"tensor": lax.rem(me + d, peers)}, device_id_type=MESH
        )

    @pl.when(has_prev)
    def _():
        pl.semaphore_signal(barrier, inc=1, device_id={"section": sec - 1}, device_id_type=MESH)

    @pl.when(has_next)
    def _():
        pl.semaphore_signal(barrier, inc=1, device_id={"section": sec + 1}, device_id_type=MESH)

    def acts_copy(c):
        return pltpu.make_async_copy(acts.at[0, :, :, span(c)], slots.at[:, :, span(c)], acts_sem.at[c])

    small = [
        pltpu.make_async_copy(src, dst, small_sem.at[i])
        for i, (src, dst) in enumerate([(order_h, order), (gain_h, gain), (bias_h, bias)])
    ]
    small[0].start()
    for c in range(n_chunks):
        acts_copy(c).start()
    small[1].start()
    small[2].start()

    def wi_copy(i):
        cols = pl.ds(i * wi_tile, wi_tile)
        return pltpu.make_async_copy(w_in.at[0, :, cols], wi.at[:, cols], wi_sem.at[i])

    load_wo = pltpu.make_async_copy(w_out.at[0], wo, wo_sem)
    load_fresh = pltpu.make_async_copy(fresh, fresh_v, fresh_sem)

    def ag_copy(t, d, c):
        return pltpu.make_async_remote_copy(
            src_ref=hs.at[t, 0, :, span(c)],
            dst_ref=hs.at[t, d, :, span(c)],
            send_sem=ag_send.at[t, d - 1],
            recv_sem=ag_recv.at[t, d - 1, c],
            device_id={"tensor": lax.rem(me + d, peers)},
            device_id_type=MESH,
        )

    def rs_copy(t, d, c):
        return pltpu.make_async_remote_copy(
            src_ref=part.at[t, d, :, part_span(c)],
            dst_ref=got.at[t, d - 1, :, part_span(c)],
            send_sem=rs_send.at[t, d - 1],
            recv_sem=rs_recv.at[t, d - 1, c],
            device_id={"tensor": lax.rem(me - d + peers, peers)},
            device_id_type=MESH,
        )

    def hop_copy(t, c):
        return pltpu.make_async_remote_copy(
            src_ref=out.at[t, 0, :, part_span(c)],
            dst_ref=arr.at[t, :, part_span(c)],
            send_sem=hop_send.at[t],
            recv_sem=hop_recv.at[t, c],
            device_id={"section": lax.rem(sec + 1, sections)},
            device_id_type=MESH,
        )

    def yield_turn(i, when):
        partner = sec + 1 - 2 * lax.rem(sec, 2)

        @pl.when(when)
        def _():
            pl.semaphore_signal(
                turn.at[i], inc=1, device_id={"section": partner}, device_id_type=MESH
            )

    def await_turn(i):
        with jax.named_scope(f"turn_{i}"):
            pl.semaphore_wait(turn.at[i], 1)

    def pieces(step):
        for i in range(rows // PIECE):
            step(pl.ds(i * PIECE, PIECE))

    def pick(t, values):
        chosen = order[0, t]
        x = values[0]
        for k in range(1, n_slots):
            x = jnp.where(chosen == k, values[k], x)
        return x

    def offer(t, c):
        def step(r):
            values = [slots[k, r, span(c)].astype(jnp.float32) for k in range(n_slots)]
            xs[t, r, span(c)] = pick(t, values).astype(jnp.bfloat16)

        pieces(step)

    def send_rows(t):
        for c in range(n_chunks):
            for d in range(1, peers):
                ag_copy(t, d, c).start()

    def norm(t):
        g = gain[0:1, :]
        b = bias[0:1, :]

        def one(i, carry):
            r = pl.ds(pl.multiple_of(i * NORM_ROWS, NORM_ROWS), NORM_ROWS)
            values = xs[t, r, :].astype(jnp.float32)
            centred = values - jnp.mean(values, axis=-1, keepdims=True)
            spread = jnp.mean(centred * centred, axis=-1, keepdims=True)
            hs[t, 0, r, :] = (centred * lax.rsqrt(spread + EPS) * g + b).astype(jnp.bfloat16)
            return carry

        lax.fori_loop(0, rows // NORM_ROWS, one, 0, unroll=4)

    def project(t):
        for i in range(n_tiles):
            if t == 0:
                wi_copy(i).wait()
            cols = pl.ds(i * wi_tile, wi_tile)
            y = jnp.dot(hs[t, 0], wi[:, cols], preferred_element_type=jnp.float32)
            qkv[0:rows, cols] = y.astype(jnp.bfloat16)

    def project_chunk(t, d, c):
        for i in range(n_tiles):
            cols = pl.ds(i * wi_tile, wi_tile)
            y = jnp.dot(
                hs[t, d, :, span(c)], wi[span(c), cols], preferred_element_type=jnp.float32
            )
            if c:
                y = acc[:, cols] + y
            if c + 1 < n_chunks:
                acc[:, cols] = y
            else:
                qkv[d * rows:(d + 1) * rows, cols] = y.astype(jnp.bfloat16)

    scale = math.log2(math.e) / math.sqrt(HD)

    def attend(t, d):
        r = slice(d * rows, (d + 1) * rows)
        for n in range(heads):
            base = n * 3 * HD
            q = qkv[r, base:base + HD]
            k = qkv[:, base + HD:base + 2 * HD]
            v = qkv[:, base + 2 * HD:base + 3 * HD]
            s = lax.dot_general(q, k, (((1,), (1,)), ((), ())), preferred_element_type=jnp.float32)
            e = jnp.exp2((s - jnp.max(s, axis=-1, keepdims=True)) * scale)
            total = jnp.sum(e, axis=-1, keepdims=True)
            y = jnp.dot(e.astype(jnp.bfloat16), v, preferred_element_type=jnp.float32)
            mixed[:, n * HD:(n + 1) * HD] = (y / total).astype(jnp.bfloat16)

        for c in range(n_parts):
            with jax.named_scope(f"wo_{t}_{d}_{c}"):
                y = jnp.dot(mixed[...], wo[:, part_span(c)], preferred_element_type=jnp.float32)
                part[t, d, :, part_span(c)] = y.astype(jnp.bfloat16)
                if d == 1 and c == 0:
                    @pl.when(late)
                    def _():
                        await_turn(1 + 2 * t)
                if d:
                    rs_copy(t, d, c).start()

    def finish(t):
        for c in range(n_parts):
            with jax.named_scope(f"rs_wait_{t}_{c}"):
                for d in range(1, peers):
                    rs_copy(t, d, c).wait_recv()
            if t == 0 and c == min(1, n_parts - 1):
                yield_turn(1, leads)

            def step(r):
                total = part[t, 0, r, part_span(c)].astype(jnp.float32)
                for d in range(1, peers):
                    total = total + got[t, d - 1, r, part_span(c)].astype(jnp.float32)
                x = xs[t, r, part_span(c)].astype(jnp.float32)
                out[t, 0, r, part_span(c)] = (x + total).astype(jnp.bfloat16)

            pieces(step)

            @pl.when(has_next)
            def _():
                hop_copy(t, c).start()

    def take(t):
        chosen = order[0, t]
        last = t + 1 == ticks

        def step(r, source, c):
            new = source[t, r, part_span(c)].astype(jnp.float32)
            values = [
                jnp.where(chosen == k, new, slots[k, r, part_span(c)].astype(jnp.float32))
                for k in range(n_slots)
            ]
            for k in range(n_slots):
                if last:
                    held[0, k, r, part_span(c)] = values[k].astype(jnp.bfloat16)
                else:
                    slots[k, r, part_span(c)] = values[k].astype(jnp.bfloat16)
            if not last:
                xs[t + 1, r, part_span(c)] = pick(t + 1, values).astype(jnp.bfloat16)

        for c in range(n_parts):
            @pl.when(has_prev)
            def _():
                with jax.named_scope(f"hop_wait_{t}_{c}"):
                    hop_copy(t, c).wait_recv()
                pieces(functools.partial(step, source=arr, c=c))

            @pl.when(jnp.logical_not(has_prev))
            def _():
                pieces(functools.partial(step, source=fresh_v, c=c))

    small[0].wait()
    for c in range(n_chunks):
        acts_copy(c).wait()
        if c + 1 == n_chunks:
            for i in range(n_tiles):
                wi_copy(i).start()
            load_wo.start()
            load_fresh.start()
        offer(0, c)
    small[1].wait()
    small[2].wait()
    with jax.named_scope("norm_first"):
        norm(0)
    with jax.named_scope("barrier"):
        pl.semaphore_wait(
            barrier, peers - 1 + has_prev.astype(jnp.int32) + has_next.astype(jnp.int32)
        )

    @pl.when(early)
    def _():
        send_rows(0)

    with jax.named_scope("project_first"):
        project(0)

    @pl.when(late)
    def _():
        await_turn(0)
        send_rows(0)

    for t in range(ticks):
        for d in range(1, peers):
            for c in range(n_chunks):
                with jax.named_scope(f"ag_wait_{t}_{c}"):
                    ag_copy(t, d, c).wait_recv()
                if d == 1 and c == min(1, n_chunks - 1):
                    yield_turn(3 * t, leads)
                    if t:
                        yield_turn(2, late)
                with jax.named_scope(f"pchunk_{t}_{c}"):
                    project_chunk(t, d, c)
        if t == 0:
            load_wo.wait()
        for d in [*range(1, peers), 0]:
            with jax.named_scope(f"attend_{t}_{d}"):
                attend(t, d)
        if t == 0:
            load_fresh.wait()
        if t + 1 == ticks:
            finish(t)
            take(t)
        else:
            @pl.when(early)
            def _():
                finish(t)

            take(t)
            with jax.named_scope(f"norm_{t}"):
                norm(t + 1)

            @pl.when(leads)
            def _():
                await_turn(2)

            send_rows(t + 1)

            @pl.when(late)
            def _():
                finish(t)

            with jax.named_scope(f"project_{t}"):
                project(t + 1)

    for t in range(ticks):
        for d in range(1, peers):
            for sem in (ag_send, rs_send):
                pltpu.make_async_copy(hs.at[t, 0], hs.at[t, 0], sem.at[t, d - 1]).wait()

        @pl.when(has_next)
        def _():
            pltpu.make_async_copy(hs.at[t, 0], hs.at[t, 0], hop_send.at[t]).wait()


def flush(out_v, held_v, out, held, sem):
    copies = [
        pltpu.make_async_copy(out_v, out, sem.at[0]),
        pltpu.make_async_copy(held_v, held, sem.at[1]),
    ]
    for copy in copies:
        copy.start()
    for copy in copies:
        copy.wait()


def pin(*xs):
    return [pltpu.with_memory_space_constraint(x, pltpu.HBM) for x in xs]


def body(acts, fresh, order, ln_gain, ln_bias, wqkv, wo):
    ticks, rows, width = fresh.shape
    n_slots = acts.shape[1]
    peers = lax.axis_size("tensor")
    seq = rows * peers
    n_chunks = width // fitting(CHUNK, width)
    n_parts = len(rs_spans(width))
    inner = wo.shape[1]
    wide = wqkv.shape[2]
    bf = jnp.bfloat16
    dma = pltpu.SemaphoreType.DMA
    anywhere = pl.BlockSpec(memory_space=pl.ANY)
    vmem = pl.BlockSpec(memory_space=pltpu.VMEM)
    out_shape = (ticks, 1, rows, width)
    held_shape = (1, n_slots, rows, width)
    results = pl.pallas_call(
        relay,
        out_shape=(pltpu.VMEM(out_shape, bf), pltpu.VMEM(held_shape, bf)),
        in_specs=[anywhere] * 7,
        out_specs=(vmem, vmem),
        scratch_shapes=[
            pltpu.SMEM(order.shape, jnp.int32),
            pltpu.VMEM(ln_gain.shape, jnp.float32),
            pltpu.VMEM(ln_bias.shape, jnp.float32),
            pltpu.VMEM((n_slots, rows, width), bf),
            pltpu.VMEM((ticks, rows, width), bf),
            pltpu.VMEM((width, wide), bf),
            pltpu.VMEM((inner, width), bf),
            pltpu.VMEM((ticks, rows, width), bf),
            pltpu.VMEM((ticks, peers, rows, width), bf),
            pltpu.VMEM((rows, wide), jnp.float32),
            pltpu.VMEM((seq, wide), bf),
            pltpu.VMEM((rows, inner), bf),
            pltpu.VMEM((ticks, peers, rows, width), bf),
            pltpu.VMEM((ticks, peers - 1, rows, width), bf),
            pltpu.VMEM((ticks, rows, width), bf),
            dma((3,)),
            dma((n_chunks,)),
            dma,
            dma((wide // fitting(TILE, wide),)),
            dma,
            dma((ticks, peers - 1)),
            dma((ticks, peers - 1, n_chunks)),
            dma((ticks, peers - 1)),
            dma((ticks, peers - 1, n_parts)),
            dma((ticks,)),
            dma((ticks, n_parts)),
            pltpu.SemaphoreType.REGULAR((4,)),
        ],
        compiler_params=pltpu.CompilerParams(
            collective_id=0, has_side_effects=True, vmem_limit_bytes=52 * 1024 * 1024
        ),
    )(*pin(acts, fresh, order, ln_gain, ln_bias, wqkv, wo))
    return pl.pallas_call(
        flush,
        out_shape=(jax.ShapeDtypeStruct(out_shape, bf), jax.ShapeDtypeStruct(held_shape, bf)),
        in_specs=[vmem, vmem],
        out_specs=(pl.BlockSpec(memory_space=pltpu.HBM), pl.BlockSpec(memory_space=pltpu.HBM)),
        scratch_shapes=[dma((2,))],
    )(*[pltpu.with_memory_space_constraint(x, pltpu.VMEM) for x in results])


def solution(mesh):
    return jax.shard_map(
        body,
        mesh=mesh,
        in_specs=(
            P("section", "dp", "tensor", None),
            P("dp", "tensor", None),
            P("section", None),
            P("section", None),
            P("section", None),
            P("section", None, "tensor"),
            P("section", "tensor", None),
        ),
        out_specs=(P("dp", "section", "tensor", None), P("section", "dp", "tensor", None)),
        check_vma=False,
    )
```

time: 64.9 us -> 55.7 us (0.86)
  Pallas kernels: 62.1 us -> 54 us
  local copies, waits for them, and re-layouts: 1.94 us -> 0 us
    pallas_call x1 -> x2, Pallas kernels: 62.1 us -> 54 us  [the longest x1 52.7 us: body(): pl.pallas_call(relay, out_shape=(pltpu.VMEM(out_shape, bf), pltpu.VMEM(he...]
    unnamed x2 -> x0, local copies, waits for them, and re-layouts: 1.94 us -> none
where the time goes in v1:
time: 55.7 us; the launch traced here: 54.8 us
  Pallas kernels  54 us (97%)
  between operations  0.8 us (1%)
    pallas_call x1, Pallas kernels, body(): pl.pallas_call(relay, out_shape=(pltpu.VMEM(out_shape, bf), pltpu.VMEM(he...  52.7 us
    pallas_call x1, Pallas kernels, body(): pl.pallas_call(flush, out_shape=(jax.ShapeDtypeStruct(out_shape, bf), jax...  1.33 us

profile of v1, /device:TPU:0, one launch (start us, length us, event | category | flops | bytes accessed | tf_op | source)
XLA Modules:
  0.0 54.8 jit_solution(7793552273290271352)
XLA Ops:
  0.6 52.7 %shard_map.86 = (bf16[2,1,128,2048]{3,2,1,0:T(8,128)(2,1)S(1)}, bf16[1,2,128,2048]{3,2,1,0:T(8,128)(2,1)S(1)}) custom-call(bf16[1,2,128,2048]{3,2,1,0:T(8,128)(2,1)} %acts.1, bf16[2,128,2048]{2,1,0:T(8,128)(2,1)} %fresh.1, s32[1,2]{1,0:T(1,128)} %order_h.1, f32[1,2048]{1,0:T(1,128)} %gain_h.1, f32[1,2048]{1,0:T(1,128)} %bias_h.1, ...), custom_call_target="tpu_custom_call" | custom-call | tf_op jit(solution)/shard_map/pallas_call | solution.py:386
  53.3 1.3 %shard_map.87 = (bf16[2,1,128,2048]{3,2,1,0:T(8,128)(2,1)}, bf16[1,2,128,2048]{3,2,1,0:T(8,128)(2,1)}) custom-call(bf16[2,1,128,2048]{3,2,1,0:T(8,128)(2,1)S(1)} %get-tuple-element.4.out_v, bf16[1,2,128,2048]{3,2,1,0:T(8,128)(2,1)S(1)} %get-tuple-element.5.held_v), custom_call_target="tpu_custom_call" | custom-call | tf_op jit(solution)/shard_map/pallas_call | solution.py:424

commit v2 on v1

--- a/solution.py
+++ b/solution.py
@@ -21,11 +21,22 @@
     return math.gcd(most, size)
 
 
+def spans(sizes):
+    return [(sum(sizes[:i]), size) for i, size in enumerate(sizes)]
+
+
+def ag_spans(width):
+    chunk = fitting(CHUNK, width)
+    half = chunk // 2
+    if width < 2 * chunk:
+        return spans([chunk])
+    return spans([chunk] * (width // chunk - 2) + [half, chunk, half])
+
+
 def rs_spans(width):
     chunk = fitting(CHUNK, width)
-    half = fitting(chunk // 2, width)
-    sizes = [chunk] * (width // chunk - 1) + [half] * (chunk // half)
-    return [(sum(sizes[:i]), size) for i, size in enumerate(sizes)]
+    half = chunk // 2
+    return spans([chunk] * (width // chunk - 1) + [half, half])
 
 
 def relay(
@@ -41,8 +52,6 @@
     me = lax.axis_index("tensor")
     sec = lax.axis_index("section")
     heads = wi.shape[1] // (3 * HD)
-    chunk = fitting(CHUNK, width)
-    n_chunks = width // chunk
     wi_tile = fitting(TILE, wi.shape[1])
     n_tiles = wi.shape[1] // wi_tile
     has_prev = sec > 0
@@ -50,11 +59,15 @@
     late = lax.rem(sec, 2) == 1
     early = jnp.logical_not(late)
     leads = early & has_next
+    chunks = ag_spans(width)
+    n_chunks = len(chunks)
+    n_lead = max(1, n_chunks - 2)
+    lead_cols = sum(size for _, size in chunks[:n_lead])
     parts = rs_spans(width)
     n_parts = len(parts)
 
     def span(c):
-        return pl.ds(c * chunk, chunk)
+        return pl.ds(*chunks[c])
 
     def part_span(c):
         return pl.ds(*parts[c])
@@ -97,7 +110,7 @@
         return pltpu.make_async_remote_copy(
             src_ref=hs.at[t, 0, :, span(c)],
             dst_ref=hs.at[t, d, :, span(c)],
-            send_sem=ag_send.at[t, d - 1],
+            send_sem=ag_send.at[t, d - 1, int(c >= n_lead)],
             recv_sem=ag_recv.at[t, d - 1, c],
             device_id={"tensor": lax.rem(me + d, peers)},
             device_id_type=MESH,
@@ -153,6 +166,11 @@
             xs[t, r, span(c)] = pick(t, values).astype(jnp.bfloat16)
 
         pieces(step)
+
+    def sent(t, d, tail):
+        cols = pl.ds(lead_cols, width - lead_cols) if tail else pl.ds(0, lead_cols)
+        rows_sent = hs.at[t, 0, :, cols]
+        pltpu.make_async_copy(rows_sent, rows_sent, ag_send.at[t, d - 1, tail]).wait()
 
     def send_rows(t):
         for c in range(n_chunks):
@@ -220,32 +238,31 @@
                 if d:
                     rs_copy(t, d, c).start()
 
-    def finish(t):
-        for c in range(n_parts):
-            with jax.named_scope(f"rs_wait_{t}_{c}"):
-                for d in range(1, peers):
-                    rs_copy(t, d, c).wait_recv()
-            if t == 0 and c == min(1, n_parts - 1):
-                yield_turn(1, leads)
-
-            def step(r):
-                total = part[t, 0, r, part_span(c)].astype(jnp.float32)
-                for d in range(1, peers):
-                    total = total + got[t, d - 1, r, part_span(c)].astype(jnp.float32)
-                x = xs[t, r, part_span(c)].astype(jnp.float32)
-                out[t, 0, r, part_span(c)] = (x + total).astype(jnp.bfloat16)
-
-            pieces(step)
-
-            @pl.when(has_next)
-            def _():
-                hop_copy(t, c).start()
-
-    def take(t):
+    def finish(t, c):
+        with jax.named_scope(f"rs_wait_{t}_{c}"):
+            for d in range(1, peers):
+                rs_copy(t, d, c).wait_recv()
+        if t == 0 and c == min(1, n_parts - 1):
+            yield_turn(1, leads)
+
+        def step(r):
+            total = part[t, 0, r, part_span(c)].astype(jnp.float32)
+            for d in range(1, peers):
+                total = total + got[t, d - 1, r, part_span(c)].astype(jnp.float32)
+            x = xs[t, r, part_span(c)].astype(jnp.float32)
+            out[t, 0, r, part_span(c)] = (x + total).astype(jnp.bfloat16)
+
+        pieces(step)
+
+        @pl.when(has_next)
+        def _():
+            hop_copy(t, c).start()
+
+    def take(t, c):
         chosen = order[0, t]
         last = t + 1 == ticks
 
-        def step(r, source, c):
+        def step(r, source):
             new = source[t, r, part_span(c)].astype(jnp.float32)
             values = [
                 jnp.where(chosen == k, new, slots[k, r, part_span(c)].astype(jnp.float32))
@@ -259,16 +276,15 @@
             if not last:
                 xs[t + 1, r, part_span(c)] = pick(t + 1, values).astype(jnp.bfloat16)
 
-        for c in range(n_parts):
-            @pl.when(has_prev)
-            def _():
-                with jax.named_scope(f"hop_wait_{t}_{c}"):
-                    hop_copy(t, c).wait_recv()
-                pieces(functools.partial(step, source=arr, c=c))
-
-            @pl.when(jnp.logical_not(has_prev))
-            def _():
-                pieces(functools.partial(step, source=fresh_v, c=c))
+        @pl.when(has_prev)
+        def _():
+            with jax.named_scope(f"hop_wait_{t}_{c}"):
+                hop_copy(t, c).wait_recv()
+            pieces(functools.partial(step, source=arr))
+
+        @pl.when(jnp.logical_not(has_prev))
+        def _():
+            pieces(functools.partial(step, source=fresh_v))
 
     small[0].wait()
     for c in range(n_chunks):
@@ -301,16 +317,24 @@
         send_rows(0)
 
     for t in range(ticks):
+        if t:
+            @pl.when(leads)
+            def _():
+                with jax.named_scope(f"lead_{t}"):
+                    for d in range(1, peers):
+                        sent(t, d, 0)
+
+            yield_turn(3, leads)
         for d in range(1, peers):
             for c in range(n_chunks):
                 with jax.named_scope(f"ag_wait_{t}_{c}"):
                     ag_copy(t, d, c).wait_recv()
-                if d == 1 and c == min(1, n_chunks - 1):
-                    yield_turn(3 * t, leads)
-                    if t:
-                        yield_turn(2, late)
+                if t and d == 1 and c == min(1, n_chunks - 1):
+                    yield_turn(2, late)
                 with jax.named_scope(f"pchunk_{t}_{c}"):
                     project_chunk(t, d, c)
+                if t == 0 and d == 1 and c == 0:
+                    yield_turn(0, leads)
         if t == 0:
             load_wo.wait()
         for d in [*range(1, peers), 0]:
@@ -319,14 +343,27 @@
         if t == 0:
             load_fresh.wait()
         if t + 1 == ticks:
-            finish(t)
-            take(t)
+            for c in range(n_parts):
+                finish(t, c)
+            for c in range(n_parts):
+                take(t, c)
         else:
+            ahead = max(n_parts - 3, 0)
+
             @pl.when(early)
             def _():
-                finish(t)
-
-            take(t)
+                for c in range(n_parts):
+                    finish(t, c)
+                for c in range(n_parts):
+                    take(t, c)
+
+            @pl.when(late)
+            def _():
+                for c in range(n_parts):
+                    take(t, c)
+                    if 0 <= c - 2 < ahead:
+                        finish(t, c - 2)
+
             with jax.named_scope(f"norm_{t}"):
                 norm(t + 1)
 
@@ -338,15 +375,23 @@
 
             @pl.when(late)
             def _():
-                finish(t)
+                for c in range(ahead, n_parts):
+                    finish(t, c)
 
             with jax.named_scope(f"project_{t}"):
                 project(t + 1)
 
     for t in range(ticks):
         for d in range(1, peers):
-            for sem in (ag_send, rs_send):
-                pltpu.make_async_copy(hs.at[t, 0], hs.at[t, 0], sem.at[t, d - 1]).wait()
+            if t:
+                @pl.when(jnp.logical_not(leads))
+                def _():
+                    sent(t, d, 0)
+            else:
+                sent(t, d, 0)
+            if n_lead < n_chunks:
+                sent(t, d, 1)
+            pltpu.make_async_copy(hs.at[t, 0], hs.at[t, 0], rs_send.at[t, d - 1]).wait()
 
         @pl.when(has_next)
         def _():
@@ -373,7 +418,7 @@
     n_slots = acts.shape[1]
     peers = lax.axis_size("tensor")
     seq = rows * peers
-    n_chunks = width // fitting(CHUNK, width)
+    n_chunks = len(ag_spans(width))
     n_parts = len(rs_spans(width))
     inner = wo.shape[1]
     wide = wqkv.shape[2]
@@ -409,7 +454,7 @@
             dma,
             dma((wide // fitting(TILE, wide),)),
             dma,
-            dma((ticks, peers - 1)),
+            dma((ticks, peers - 1, 2)),
             dma((ticks, peers - 1, n_chunks)),
             dma((ticks, peers - 1)),
             dma((ticks, peers - 1, n_parts)),

time: 55.7 us -> 55 us (0.987); the launches traced: 54.8 us -> 54.8 us
  no operation moved by 1% of the time
where the time goes in v2:
time: 55 us; the launch traced here: 54.8 us
  Pallas kernels  54 us (98%)
  between operations  0.8 us (1%)
    pallas_call x1, Pallas kernels, body(): pl.pallas_call(relay, out_shape=(pltpu.VMEM(out_shape, bf), pltpu.VMEM(he...  52.7 us
    pallas_call x1, Pallas kernels, body(): pl.pallas_call(flush, out_shape=(jax.ShapeDtypeStruct(out_shape, bf), jax...  1.33 us

profile of v2, /device:TPU:0, one launch (start us, length us, event | category | flops | bytes accessed | tf_op | source)
XLA Modules:
  0.0 54.8 jit_solution(10431850868764494642)
XLA Ops:
  0.6 52.7 %shard_map.86 = (bf16[2,1,128,2048]{3,2,1,0:T(8,128)(2,1)S(1)}, bf16[1,2,128,2048]{3,2,1,0:T(8,128)(2,1)S(1)}) custom-call(bf16[1,2,128,2048]{3,2,1,0:T(8,128)(2,1)} %acts.1, bf16[2,128,2048]{2,1,0:T(8,128)(2,1)} %fresh.1, s32[1,2]{1,0:T(1,128)} %order_h.1, f32[1,2048]{1,0:T(1,128)} %gain_h.1, f32[1,2048]{1,0:T(1,128)} %bias_h.1, ...), custom_call_target="tpu_custom_call" | custom-call | tf_op jit(solution)/shard_map/pallas_call | solution.py:431
  53.4 1.3 %shard_map.87 = (bf16[2,1,128,2048]{3,2,1,0:T(8,128)(2,1)}, bf16[1,2,128,2048]{3,2,1,0:T(8,128)(2,1)}) custom-call(bf16[2,1,128,2048]{3,2,1,0:T(8,128)(2,1)S(1)} %get-tuple-element.4.out_v, bf16[1,2,128,2048]{3,2,1,0:T(8,128)(2,1)S(1)} %get-tuple-element.5.held_v), custom_call_target="tpu_custom_call" | custom-call | tf_op jit(solution)/shard_map/pallas_call | solution.py:469

commit v3 on v2

--- a/solution.py
+++ b/solution.py
@@ -30,18 +30,18 @@
     half = chunk // 2
     if width < 2 * chunk:
         return spans([chunk])
-    return spans([chunk] * (width // chunk - 2) + [half, chunk, half])
+    return spans([chunk + half] + [chunk] * (width // chunk - 2) + [half])
 
 
 def rs_spans(width):
     chunk = fitting(CHUNK, width)
-    half = chunk // 2
-    return spans([chunk] * (width // chunk - 1) + [half, half])
+    tail = chunk // 4
+    return spans([chunk] * (width // chunk - 1) + [chunk - tail, tail])
 
 
 def relay(
     acts, fresh, order_h, gain_h, bias_h, w_in, w_out, out, held,
-    order, gain, bias, slots, fresh_v, wi, wo, xs, hs, acc, qkv, mixed, part, got, arr,
+    order, affine, slots, fresh_v, wi, wo, xs, hs, acc, qkv, mixed, part, got, arr,
     small_sem, acts_sem, fresh_sem, wi_sem, wo_sem,
     ag_send, ag_recv, rs_send, rs_recv, hop_send, hop_recv, turn,
 ):
@@ -61,8 +61,8 @@
     leads = early & has_next
     chunks = ag_spans(width)
     n_chunks = len(chunks)
-    n_lead = max(1, n_chunks - 2)
-    lead_cols = sum(size for _, size in chunks[:n_lead])
+    halves = 2
+    block = rows // halves
     parts = rs_spans(width)
     n_parts = len(parts)
 
@@ -86,18 +86,21 @@
     def _():
         pl.semaphore_signal(barrier, inc=1, device_id={"section": sec + 1}, device_id_type=MESH)
 
-    def acts_copy(c):
-        return pltpu.make_async_copy(acts.at[0, :, :, span(c)], slots.at[:, :, span(c)], acts_sem.at[c])
-
-    small = [
-        pltpu.make_async_copy(src, dst, small_sem.at[i])
-        for i, (src, dst) in enumerate([(order_h, order), (gain_h, gain), (bias_h, bias)])
-    ]
-    small[0].start()
-    for c in range(n_chunks):
-        acts_copy(c).start()
-    small[1].start()
-    small[2].start()
+    def row_block(i):
+        return pl.ds(i * block, block)
+
+    def acts_copy(i):
+        return pltpu.make_async_copy(
+            acts.at[0, :, row_block(i)], slots.at[:, row_block(i)], acts_sem.at[i]
+        )
+
+    load_order = pltpu.make_async_copy(order_h, order, small_sem.at[0])
+    load_order.start()
+    acts_copy(0).start()
+    pltpu.make_async_copy(gain_h, affine.at[0:1], small_sem.at[1]).start()
+    pltpu.make_async_copy(bias_h, affine.at[1:2], small_sem.at[1]).start()
+    for i in range(1, halves):
+        acts_copy(i).start()
 
     def wi_copy(i):
         cols = pl.ds(i * wi_tile, wi_tile)
@@ -106,11 +109,11 @@
     load_wo = pltpu.make_async_copy(w_out.at[0], wo, wo_sem)
     load_fresh = pltpu.make_async_copy(fresh, fresh_v, fresh_sem)
 
-    def ag_copy(t, d, c):
+    def ag_copy(t, d, c, r=slice(None), tail=0):
         return pltpu.make_async_remote_copy(
-            src_ref=hs.at[t, 0, :, span(c)],
-            dst_ref=hs.at[t, d, :, span(c)],
-            send_sem=ag_send.at[t, d - 1, int(c >= n_lead)],
+            src_ref=hs.at[t, 0, r, span(c)],
+            dst_ref=hs.at[t, d, r, span(c)],
+            send_sem=ag_send.at[t, d - 1, tail],
             recv_sem=ag_recv.at[t, d - 1, c],
             device_id={"tensor": lax.rem(me + d, peers)},
             device_id_type=MESH,
@@ -142,12 +145,12 @@
         @pl.when(when)
         def _():
             pl.semaphore_signal(
-                turn.at[i], inc=1, device_id={"section": partner}, device_id_type=MESH
+                turn.at[0], inc=1, device_id={"section": partner}, device_id_type=MESH
             )
 
     def await_turn(i):
         with jax.named_scope(f"turn_{i}"):
-            pl.semaphore_wait(turn.at[i], 1)
+            pl.semaphore_wait(turn.at[0], 1)
 
     def pieces(step):
         for i in range(rows // PIECE):
@@ -160,36 +163,43 @@
             x = jnp.where(chosen == k, values[k], x)
         return x
 
-    def offer(t, c):
-        def step(r):
-            values = [slots[k, r, span(c)].astype(jnp.float32) for k in range(n_slots)]
-            xs[t, r, span(c)] = pick(t, values).astype(jnp.bfloat16)
-
-        pieces(step)
-
-    def sent(t, d, tail):
-        cols = pl.ds(lead_cols, width - lead_cols) if tail else pl.ds(0, lead_cols)
-        rows_sent = hs.at[t, 0, :, cols]
-        pltpu.make_async_copy(rows_sent, rows_sent, ag_send.at[t, d - 1, tail]).wait()
-
-    def send_rows(t):
+    def send_rows(t, i):
+        r = row_block(i)
         for c in range(n_chunks):
             for d in range(1, peers):
-                ag_copy(t, d, c).start()
-
-    def norm(t):
-        g = gain[0:1, :]
-        b = bias[0:1, :]
-
-        def one(i, carry):
-            r = pl.ds(pl.multiple_of(i * NORM_ROWS, NORM_ROWS), NORM_ROWS)
-            values = xs[t, r, :].astype(jnp.float32)
+                ag_copy(t, d, c, r, int(i + 1 == halves and c > 0)).start()
+
+    def sent(t, d, tail):
+        def drain(r, cols):
+            copied = hs.at[t, 0, r, cols]
+            pltpu.make_async_copy(copied, copied, ag_send.at[t, d - 1, tail]).wait()
+
+        first = chunks[0][1]
+        if tail:
+            if first < width:
+                drain(row_block(halves - 1), pl.ds(first, width - first))
+        else:
+            drain(pl.ds(0, block * (halves - 1)), pl.ds(0, width))
+            drain(row_block(halves - 1), pl.ds(0, first))
+
+    def norm(t, i):
+        g = affine[0:1, :]
+        b = affine[1:2, :]
+        step = fitting(NORM_ROWS, block)
+
+        def one(n, carry):
+            r = pl.ds(pl.multiple_of(i * block + n * step, step), step)
+            if t:
+                values = xs[t, r, :].astype(jnp.float32)
+            else:
+                values = pick(t, [slots[k, r, :].astype(jnp.float32) for k in range(n_slots)])
+                xs[t, r, :] = values.astype(jnp.bfloat16)
             centred = values - jnp.mean(values, axis=-1, keepdims=True)
             spread = jnp.mean(centred * centred, axis=-1, keepdims=True)
             hs[t, 0, r, :] = (centred * lax.rsqrt(spread + EPS) * g + b).astype(jnp.bfloat16)
             return carry
 
-        lax.fori_loop(0, rows // NORM_ROWS, one, 0, unroll=4)
+        lax.fori_loop(0, block // step, one, 0, unroll=block // step)
 
     def project(t):
         for i in range(n_tiles):
@@ -286,27 +296,32 @@
         def _():
             pieces(functools.partial(step, source=fresh_v))
 
-    small[0].wait()
-    for c in range(n_chunks):
-        acts_copy(c).wait()
-        if c + 1 == n_chunks:
-            for i in range(n_tiles):
-                wi_copy(i).start()
-            load_wo.start()
-            load_fresh.start()
-        offer(0, c)
-    small[1].wait()
-    small[2].wait()
-    with jax.named_scope("norm_first"):
-        norm(0)
+    def first_rows(i):
+        with jax.named_scope(f"acts_wait_{i}"):
+            acts_copy(i).wait()
+            if i + 1 == halves:
+                for n in range(n_tiles):
+                    wi_copy(n).start()
+                load_wo.start()
+                load_fresh.start()
+        with jax.named_scope(f"norm_first_{i}"):
+            norm(0, i)
+
+    with jax.named_scope("small_wait"):
+        load_order.wait()
+        pltpu.make_async_copy(affine, affine, small_sem.at[1]).wait()
+    first_rows(0)
     with jax.named_scope("barrier"):
         pl.semaphore_wait(
             barrier, peers - 1 + has_prev.astype(jnp.int32) + has_next.astype(jnp.int32)
         )
-
-    @pl.when(early)
-    def _():
-        send_rows(0)
+    for i in range(halves):
+        if i:
+            first_rows(i)
+
+        @pl.when(early)
+        def _():
+            send_rows(0, i)
 
     with jax.named_scope("project_first"):
         project(0)
@@ -314,27 +329,25 @@
     @pl.when(late)
     def _():
         await_turn(0)
-        send_rows(0)
+        for i in range(halves):
+            send_rows(0, i)
+
+    yield_turn(0, leads)
 
     for t in range(ticks):
         if t:
-            @pl.when(leads)
-            def _():
-                with jax.named_scope(f"lead_{t}"):
-                    for d in range(1, peers):
-                        sent(t, d, 0)
+            with jax.named_scope(f"lead_{t}"):
+                for d in range(1, peers):
+                    sent(t, d, 0)
 
             yield_turn(3, leads)
+            yield_turn(2, late)
         for d in range(1, peers):
             for c in range(n_chunks):
                 with jax.named_scope(f"ag_wait_{t}_{c}"):
                     ag_copy(t, d, c).wait_recv()
-                if t and d == 1 and c == min(1, n_chunks - 1):
-                    yield_turn(2, late)
                 with jax.named_scope(f"pchunk_{t}_{c}"):
                     project_chunk(t, d, c)
-                if t == 0 and d == 1 and c == 0:
-                    yield_turn(0, leads)
         if t == 0:
             load_wo.wait()
         for d in [*range(1, peers), 0]:
@@ -364,14 +377,15 @@
                     if 0 <= c - 2 < ahead:
                         finish(t, c - 2)
 
-            with jax.named_scope(f"norm_{t}"):
-                norm(t + 1)
-
-            @pl.when(leads)
-            def _():
-                await_turn(2)
-
-            send_rows(t + 1)
+            for i in range(halves):
+                with jax.named_scope(f"norm_{t}_{i}"):
+                    norm(t + 1, i)
+                if i == 0:
+                    @pl.when(leads)
+                    def _():
+                        await_turn(2)
+
+                send_rows(t + 1, i)
 
             @pl.when(late)
             def _():
@@ -383,14 +397,9 @@
 
     for t in range(ticks):
         for d in range(1, peers):
-            if t:
-                @pl.when(jnp.logical_not(leads))
-                def _():
-                    sent(t, d, 0)
-            else:
+            if t == 0:
                 sent(t, d, 0)
-            if n_lead < n_chunks:
-                sent(t, d, 1)
+            sent(t, d, 1)
             pltpu.make_async_copy(hs.at[t, 0], hs.at[t, 0], rs_send.at[t, d - 1]).wait()
 
         @pl.when(has_next)
@@ -435,8 +444,7 @@
         out_specs=(vmem, vmem),
         scratch_shapes=[
             pltpu.SMEM(order.shape, jnp.int32),
-            pltpu.VMEM(ln_gain.shape, jnp.float32),
-            pltpu.VMEM(ln_bias.shape, jnp.float32),
+            pltpu.VMEM((2, width), jnp.float32),
             pltpu.VMEM((n_slots, rows, width), bf),
             pltpu.VMEM((ticks, rows, width), bf),
             pltpu.VMEM((width, wide), bf),
@@ -449,8 +457,8 @@
             pltpu.VMEM((ticks, peers, rows, width), bf),
             pltpu.VMEM((ticks, peers - 1, rows, width), bf),
             pltpu.VMEM((ticks, rows, width), bf),
-            dma((3,)),
-            dma((n_chunks,)),
+            dma((2,)),
+            dma((2,)),
             dma,
             dma((wide // fitting(TILE, wide),)),
             dma,
@@ -460,7 +468,7 @@
             dma((ticks, peers - 1, n_parts)),
             dma((ticks,)),
             dma((ticks, n_parts)),
-            pltpu.SemaphoreType.REGULAR((4,)),
+            pltpu.SemaphoreType.REGULAR((1,)),
         ],
         compiler_params=pltpu.CompilerParams(
             collective_id=0, has_side_effects=True, vmem_limit_bytes=52 * 1024 * 1024

time: 55 us -> 55.6 us (1.011)
  Pallas kernels: 54 us -> 54.6 us
    pallas_call x1, Pallas kernels: 52.7 us -> 53.3 us  [body(): pl.pallas_call(relay, out_shape=(pltpu.VMEM(out_shape, bf), pltpu.VMEM(he...]
where the time goes in v3:
time: 55.6 us; the launch traced here: 55.4 us
  Pallas kernels  54.6 us (98%)
  between operations  0.8 us (1%)
    pallas_call x1, Pallas kernels, body(): pl.pallas_call(relay, out_shape=(pltpu.VMEM(out_shape, bf), pltpu.VMEM(he...  53.3 us
    pallas_call x1, Pallas kernels, body(): pl.pallas_call(flush, out_shape=(jax.ShapeDtypeStruct(out_shape, bf), jax...  1.33 us

profile of v3, /device:TPU:0, one launch (start us, length us, event | category | flops | bytes accessed | tf_op | source)
XLA Modules:
  0.0 55.4 jit_solution(9678000298937653813)
XLA Ops:
  0.6 53.3 %shard_map.86 = (bf16[2,1,128,2048]{3,2,1,0:T(8,128)(2,1)S(1)}, bf16[1,2,128,2048]{3,2,1,0:T(8,128)(2,1)S(1)}) custom-call(bf16[1,2,128,2048]{3,2,1,0:T(8,128)(2,1)} %acts.1, bf16[2,128,2048]{2,1,0:T(8,128)(2,1)} %fresh.1, s32[1,2]{1,0:T(1,128)} %order_h.1, f32[1,2048]{1,0:T(1,128)} %gain_h.1, f32[1,2048]{1,0:T(1,128)} %bias_h.1, ...), custom_call_target="tpu_custom_call" | custom-call | tf_op jit(solution)/shard_map/pallas_call | solution.py:440
  53.9 1.3 %shard_map.87 = (bf16[2,1,128,2048]{3,2,1,0:T(8,128)(2,1)}, bf16[1,2,128,2048]{3,2,1,0:T(8,128)(2,1)}) custom-call(bf16[2,1,128,2048]{3,2,1,0:T(8,128)(2,1)S(1)} %get-tuple-element.4.out_v, bf16[1,2,128,2048]{3,2,1,0:T(8,128)(2,1)S(1)} %get-tuple-element.5.held_v), custom_call_target="tpu_custom_call" | custom-call | tf_op jit(solution)/shard_map/pallas_call | solution.py:477
